TPU v7x, 256 devices: a whole 4x4x8 slice. The times are simulated.
256 devices in a mesh: section: 4 (over y), fsdp: 64 (over z, x, core).
Axes of the slice: x: 4, y: 4, z: 8, core: 2. Of those that a mesh axis runs over, the one named last changes fastest.
Arguments:
- residual_input: bfloat16 [2, 4096, 8192], P(None, 'fsdp'), may hold values from -16 to 16
- output_gradient: bfloat16 [2, 4096, 8192], P(None, 'fsdp'), may hold values from -0.0068359375 to 0.0068359375
- value_projection_weight: bfloat16 [4, 8192, 512], P('section', 'fsdp'), may hold values from -0.0625 to 0.0625
- output_weight: bfloat16 [4, 512, 8192], P('section', None, 'fsdp'), may hold values from -0.25 to 0.25
- adapter_down_weight: bfloat16 [4, 8192, 160], P('section'), may hold values from -0.0625 to 0.0625
- adapter_up_weight: bfloat16 [4, 160, 512], P('section'), may hold values from -0.625 to 0.625
- input_norm_scale: float32 [4, 8192], P('section'), may hold values from 0.25 to 1.75
- segment_adapter_index: int32 [2, 128], P(None, 'fsdp'), may hold values from 0 to 3
- adapter_rank_blocks: int32 [4], replicated, may hold values from 1 to 16, 20 in all
Outputs:
- grad_down: float32 [4, 8192, 160], P('section', 'fsdp')
- grad_up: float32 [4, 160, 512], P('section', None, 'fsdp')
Inputs may be any that keep to these rules, and one draw needn't show every extreme that they name: `segment_adapter_index`: adapter of each block of 32 consecutive tokens. `adapter_rank_blocks`: the entries sum to 20.
All inputs are finite; a program needn't handle non-finite values.
Results may differ from a plain program's by a relative error of at most 0.014.
Values may be sent and summed in bfloat16 or wider, within the bound.
No kernel may reach another device: no remote copies, remote signals or barrier semaphores. Data moves between devices by JAX's collectives and lax.ppermute only.
A program may use at most 128 MiB of HBM per device.

v0:
```python
import jax
import jax.numpy as jnp
from jax import lax
from jax.experimental.layout import Layout, with_layout_constraint
from jax.sharding import Mesh, PartitionSpec as P

ADAPTERS = 4
EPSILON = 1e-06
ADAPTER_ALPHA = 32.0
BF = jnp.bfloat16
F32 = jnp.float32
GROUP = ("y", "z", "c")


def contract(left, right, left_dim, right_dim):
    return lax.dot_general(
        left, right, (((left_dim,), (right_dim,)), ((), ())), preferred_element_type=F32
    )


def split_pair(value):
    high = lax.reduce_precision(value, 8, 7)
    return (high.astype(BF), (value - high).astype(BF))


def coefficient_row(adapter, adapter_rank_blocks, columns):
    rank_sizes = 8 * adapter_rank_blocks
    adapters = jnp.arange(ADAPTERS, dtype=jnp.int32)
    ends = jnp.sum(
        jnp.where(adapters[None, :] <= adapters[:, None], rank_sizes[None, :], 0), axis=1
    )
    column = jnp.arange(columns, dtype=jnp.int32)
    owner = jnp.sum((column[:, None] >= ends[None, :]).astype(jnp.int32), axis=1)
    rank = jnp.sum(jnp.where(adapters == adapter, rank_sizes, 0)).astype(F32)
    return jnp.where(owner == adapter, ADAPTER_ALPHA / rank, 0.0)[None, :]


def exchanged(value, axis):
    return lax.all_to_all(value, axis, split_axis=0, concat_axis=0, tiled=True)


def summed(value):
    return value.astype(F32).sum(axis=0)


def gathered_sum(partial):
    return summed(lax.all_gather(partial, "x", axis=0, tiled=False))


def local(
    residual_input,
    output_gradient,
    value_projection_weight,
    output_weight,
    adapter_down_weight,
    adapter_up_weight,
    input_norm_scale,
    segment_adapter_index,
    adapter_rank_blocks,
):
    ny, nz, nx, nc = (lax.axis_size(name) for name in ("y", "z", "x", "c"))
    yi, zi, xi, ci = (lax.axis_index(name) for name in ("y", "z", "x", "c"))
    rows = value_projection_weight.shape[1]
    value_cols = value_projection_weight.shape[2]
    packed = adapter_down_weight.shape[2]
    width = adapter_down_weight.shape[1]
    both = value_cols + packed
    layers = ny
    lanes = nc * rows
    depth = nz * lanes
    joined = jnp.concatenate([value_projection_weight[0], output_weight[0].T], axis=1)
    joined = with_layout_constraint(joined, Layout(major_to_minor=(0, 1)))
    full = lax.all_gather(joined, GROUP, axis=0, tiled=False)
    full = with_layout_constraint(full, Layout(major_to_minor=(0, 1, 2)))
    full = full.reshape(layers, depth, 2 * value_cols)
    value_full = [full[layer, :, :value_cols] for layer in range(layers)]
    out_full = [full[layer, :, value_cols:] for layer in range(layers)]
    all_tokens = residual_input.shape[0] * residual_input.shape[1]
    tokens = all_tokens // ny
    first = yi * tokens
    own = jnp.stack(
        [
            lax.dynamic_slice(array.reshape(all_tokens, width), (first, 0), (tokens, width))
            for array in (residual_input, output_gradient)
        ]
    )
    own = own.reshape(2, tokens, nz, nx, lanes).transpose(3, 0, 1, 2, 4)
    spread = exchanged(own.reshape(nx, 2, tokens, depth), "x")
    state = spread[:, 0].reshape(nx * tokens, depth)
    grad = spread[:, 1].reshape(nx * tokens, depth)
    down_local = lax.dynamic_index_in_dim(
        adapter_down_weight[0].T.reshape(packed, nz, nx, lanes), xi, 2, keepdims=False
    ).reshape(1, packed, depth)
    downs_full = exchanged(jnp.broadcast_to(down_local, (layers, packed, depth)), "y")
    gains_local = lax.dynamic_index_in_dim(
        input_norm_scale.reshape(nz, nx, lanes), xi, 1, keepdims=False
    ).reshape(depth)
    gains = lax.all_gather(gains_local, "y", axis=0, tiled=False)
    ups = lax.all_gather(adapter_up_weight[0], "y", axis=0, tiled=False)
    adapter = lax.dynamic_index_in_dim(segment_adapter_index.reshape(ny), yi, 0, keepdims=False)
    coef_row = coefficient_row(adapter, adapter_rank_blocks, packed)
    coef = lax.all_gather(jnp.broadcast_to(coef_row, (tokens, packed)), "x", axis=0, tiled=True)
    chunk = value_cols // layers
    last = contract(grad, out_full[layers - 1], 1, 0).astype(BF)
    inputs, scaled, projected, inverse, last_sum = ([], [], [], [], [])
    for layer in range(layers):
        widened = state.astype(F32)
        squares = jnp.sum(widened * widened, axis=-1, keepdims=True)
        scaled_input = (widened * gains[layer][None, :]).astype(BF)
        high, low_part = split_pair(squares)
        total = gathered_sum(
            jnp.concatenate(
                [
                    contract(scaled_input, value_full[layer], 1, 0).astype(BF),
                    last[:, layer * chunk : (layer + 1) * chunk],
                    contract(scaled_input, downs_full[layer], 1, 1).astype(BF),
                    high,
                    low_part,
                ],
                axis=1,
            )
        )
        side = value_cols + chunk
        mean = (total[:, side + packed : side + packed + 1] + total[:, side + packed + 1 :]) / width
        inv = lax.rsqrt(mean + EPSILON)
        value_part, low_piece = (total[:, :value_cols], total[:, side : side + packed])
        inputs.append(state)
        scaled.append(scaled_input)
        projected.append((value_part, low_piece))
        inverse.append(inv)
        last_sum.append(total[:, value_cols:side])
        if layer + 1 < layers:
            low = (low_piece * inv * coef).astype(BF)
            value = (value_part * inv + contract(low, ups[layer], 1, 0)).astype(BF)
            state = (widened + contract(value, out_full[layer], 1, 1)).astype(BF)
    blocks = [None] * layers
    extra = -(-packed // rows)
    for layer in reversed(range(layers)):
        if layer + 1 < layers:
            value_sum = gathered_sum(contract(grad, out_full[layer], 1, 0).astype(BF))
        else:
            value_sum = jnp.concatenate(last_sum, axis=1)
        value_grad = value_sum.astype(BF)
        low_grad = (contract(value_grad, ups[layer], 1, 1) * coef).astype(BF)
        inv = inverse[layer]
        value_part, low_piece = projected[layer]
        wide_value, wide_low = (value_grad.astype(F32), low_grad.astype(F32))
        mixed_value, mixed_low = ((wide_value * inv).astype(BF), (wide_low * inv).astype(BF))
        if layer > 0:
            inner = jnp.sum(value_part * wide_value, axis=1, keepdims=True)
            inner = inner + jnp.sum(low_piece * wide_low, axis=1, keepdims=True)
            kappa = inv * inv * inv * inner / width
            back = contract(mixed_value, value_full[layer], 1, 1)
            back = back + contract(mixed_low, downs_full[layer], 1, 0)
            grad = (
                grad.astype(F32) + gains[layer][None, :] * back - kappa * inputs[layer].astype(F32)
            ).astype(BF)
        down = contract(mixed_low, scaled[layer], 0, 0)
        down = down.reshape(packed, nz, nc, rows).transpose(2, 1, 0, 3)
        low = (low_piece * inv * coef).astype(BF)
        chosen = lax.dynamic_index_in_dim(
            value_grad.reshape(nx * tokens, nz, nx, -1), xi, 2, keepdims=False
        )
        each = chosen.shape[2] // nc
        up = contract(chosen.reshape(nx * tokens, -1), low, 0, 0)
        up = up.reshape(nz, nc, each, packed).transpose(1, 0, 2, 3)
        up = jnp.pad(up, ((0, 0), (0, 0), (0, 0), (0, extra * rows - packed)))
        block = jnp.concatenate(
            [down] + [up[..., k * rows : (k + 1) * rows] for k in range(extra)], axis=2
        ).astype(BF)
        blocks[layer] = summed(exchanged(block, "c")).astype(BF)
    total = summed(exchanged(jnp.stack(blocks), "y")).astype(BF)
    total = summed(exchanged(total, "z"))
    up = jnp.concatenate(
        [total[packed + k * each : packed + (k + 1) * each] for k in range(extra)], axis=1
    )[:, :packed]
    return (total[:packed].T[None], up.T[None])


def solution(mesh):
    shape = mesh.devices.shape
    cores, across = (2, 4)
    split = Mesh(
        mesh.devices.reshape(shape[0], shape[1] // (across * cores), across, cores),
        ("y", "z", "x", "c"),
    )
    fsdp = ("z", "x", "c")
    placed = (
        P(None, fsdp, None),
        P(None, fsdp, None),
        P("y", fsdp, None),
        P("y", None, fsdp),
        P("y", None, None),
        P("y", None, None),
        P("y", None),
        P(None, fsdp),
        P(),
    )
    return jax.shard_map(
        local,
        mesh=split,
        in_specs=placed,
        out_specs=(P("y", fsdp, None), P("y", None, fsdp)),
        check_vma=False,
    )
```

profile of v0, /device:TPU:2, one launch (start us, length us, event | category | flops | bytes accessed | tf_op | source)
XLA Modules:
  0.0 391.7 jit_solution(12321162908527013947)
XLA Ops:
  14.2 5.7 %all-to-all-start = ((bf16[4,2,32,2048]{3,2,1,0:T(8,128)(2,1)}), bf16[4,2,32,2048]{3,2,1,0:T(8,128)(2,1)S(1)}, u32[]{:S(2)}, u32[]{:S(2)}) async-start(bf16[4,2,32,2048]{3,2,1,0:T(8,128)(2,1)} %reshape.261), calls=%async_computation | async-start | bytes 2097152 | tf_op jit(solution)/shard_map/all_to_all | solution.py:39
  23.8 5.5 %reshape.264 = bf16[160,8,4,256]{3,2,1,0:T(4,128)(2,1)} reshape(bf16[160,8192]{1,0:T(8,128)(2,1)} %bitcast.315) | data formatting | bytes 5242880 | tf_op jit(solution)/shard_map/reshape | solution.py:92
  29.3 5.6 %dynamic-slice_reduce_fusion = bf16[160,8,256]{2,1,0:T(8,128)(2,1)S(1)} fusion(bf16[160,8,4,256]{3,2,1,0:T(4,128)(2,1)} %reshape.264, s32[]{:T(128)S(6)} %select_n.36), kind=kLoop, calls=%fused_computation.52 | loop fusion | bytes 1310724 | tf_op jit(solution)/shard_map/jit(dynamic_index_in_dim)/dynamic_slice | solution.py:91
  36.0 13.0 %all_gather.63 = bf16[4,160,512]{2,1,0:T(8,128)(2,1)S(1)} all-gather(bf16[1,160,512]{2,1,0:T(8,128)(2,1)S(1)} %copy-done.30), channel_id=1, replica_groups=mesh['y'=4,'z'=8,'x'=4,'c'=2] {'y'}, dimensions={0}, use_global_device_ids=true | all-gather | bytes 819200 | tf_op jit(solution)/shard_map/all_gather | solution.py:99
  50.9 4.6 %all-to-all-start.1 = ((bf16[4,160,2048]{2,1,0:T(8,128)(2,1)}), bf16[4,160,2048]{2,1,0:T(8,128)(2,1)}, u32[]{:S(2)}, u32[]{:S(2)}) async-start(bf16[4,160,2048]{2,1,0:T(8,128)(2,1)} %broadcast_in_dim.35), calls=%async_computation.1 | async-start | bytes 5242880 | tf_op jit(solution)/shard_map/all_to_all | solution.py:39
  55.5 12.0 %all_gather.62 = f32[128,160]{1,0:T(8,128)S(1)} all-gather(f32[32,160]{1,0:T(8,128)S(1)} %broadcast_in_dim.65), channel_id=1, replica_groups=mesh['y'=4,'z'=8,'x'=4,'c'=2] {'x'}, dimensions={0}, use_global_device_ids=true | all-gather | bytes 102400 | tf_op jit(solution)/shard_map/all_gather | solution.py:102
  67.6 44.8 %all-gather.8 = f32[4,1,2048]{2,1,0:T(1,128)S(1)} all-gather(f32[1,1,2048]{2,1,0:T(1,128)S(1)} %bitcast.353), channel_id=1, replica_groups=mesh['y'=4,'z'=8,'x'=4,'c'=2] {'y'}, dimensions={0}, use_global_device_ids=true | all-gather | bytes 40960 | tf_op jit(solution)/shard_map/all_gather | solution.py:98
  117.5 17.1 %all-gather.11.cloned.1.call-done = bf16[8192,1024]{1,0:T(8,128)(2,1)} async-done(((bf16[128,1024]{1,0:T(8,128)(2,1)}), bf16[8192,1024]{1,0:T(8,128)(2,1)}) %all-gather.11.cloned.1.call-update) | async-done | bytes 16777232 | tf_op jit(solution)/shard_map/all_gather | solution.py:73
  139.6 14.7 %all-gather.1 = bf16[512,802]{1,0:T(8,128)(2,1)S(1)} all-gather(bf16[128,802]{1,0:T(8,128)(2,1)S(1)} %concatenate.52), channel_id=3, replica_groups=mesh['y'=4,'z'=8,'x'=4,'c'=2] {'x'}, dimensions={0}, use_global_device_ids=true | all-gather | bytes 1026560 | tf_op jit(solution)/shard_map/all_gather | solution.py:47
  154.8 3.3 multiply_reduce_fusion.2
  162.4 13.8 %all-gather.2 = bf16[512,802]{1,0:T(8,128)(2,1)S(1)} all-gather(bf16[128,802]{1,0:T(8,128)(2,1)S(1)} %concatenate.53), channel_id=4, replica_groups=mesh['y'=4,'z'=8,'x'=4,'c'=2] {'x'}, dimensions={0}, use_global_device_ids=true | all-gather | bytes 1026560 | tf_op jit(solution)/shard_map/all_gather | solution.py:47
  177.2 3.4 multiply_reduce_fusion.1
  184.8 14.2 %all-gather.3 = bf16[512,802]{1,0:T(8,128)(2,1)S(1)} all-gather(bf16[128,802]{1,0:T(8,128)(2,1)S(1)} %concatenate.54), channel_id=5, replica_groups=mesh['y'=4,'z'=8,'x'=4,'c'=2] {'x'}, dimensions={0}, use_global_device_ids=true | all-gather | bytes 1026560 | tf_op jit(solution)/shard_map/all_gather | solution.py:47
  205.6 3.5 multiply_reduce_fusion
  216.7 13.6 %all-gather.4 = bf16[512,802]{1,0:T(8,128)(2,1)S(1)} all-gather(bf16[128,802]{1,0:T(8,128)(2,1)S(1)} %concatenate.55), channel_id=6, replica_groups=mesh['y'=4,'z'=8,'x'=4,'c'=2] {'x'}, dimensions={0}, use_global_device_ids=true | all-gather | bytes 1026560 | tf_op jit(solution)/shard_map/all_gather | solution.py:47
  246.2 12.8 %all-gather.5 = bf16[512,512]{1,0:T(8,128)(2,1)S(1)} all-gather(bf16[128,512]{1,0:T(8,128)(2,1)S(1)} %fusion.34), channel_id=7, replica_groups=mesh['y'=4,'z'=8,'x'=4,'c'=2] {'x'}, dimensions={0}, use_global_device_ids=true | all-gather | bytes 655360 | tf_op jit(solution)/shard_map/all_gather | solution.py:47
  270.3 12.8 %all-gather.6 = bf16[512,512]{1,0:T(8,128)(2,1)S(1)} all-gather(bf16[128,512]{1,0:T(8,128)(2,1)S(1)} %fusion.36), channel_id=8, replica_groups=mesh['y'=4,'z'=8,'x'=4,'c'=2] {'x'}, dimensions={0}, use_global_device_ids=true | all-gather | bytes 655360 | tf_op jit(solution)/shard_map/all_gather | solution.py:47
  291.2 4.3 %all_to_all.40 = bf16[2,8,176,128]{3,1,2,0:T(8,128)(2,1)S(1)} all-to-all(bf16[2,8,176,128]{3,1,2,0:T(8,128)(2,1)S(1)} %pad_maximum_fusion.4), channel_id=1, replica_groups=mesh['y'=4,'z'=8,'x'=4,'c'=2] {'c'}, dimensions={0} | all-to-all | bytes 1441792 | tf_op jit(solution)/shard_map/all_to_all | solution.py:39
  301.8 4.5 %all_to_all.41 = bf16[2,8,176,128]{3,1,2,0:T(8,128)(2,1)S(1)} all-to-all(bf16[2,8,176,128]{3,1,2,0:T(8,128)(2,1)S(1)} %pad_maximum_fusion.3), channel_id=1, replica_groups=mesh['y'=4,'z'=8,'x'=4,'c'=2] {'c'}, dimensions={0} | all-to-all | bytes 1441792 | tf_op jit(solution)/shard_map/all_to_all | solution.py:39
  314.1 4.3 %all_to_all.42 = bf16[2,8,176,128]{3,1,2,0:T(8,128)(2,1)S(1)} all-to-all(bf16[2,8,176,128]{3,1,2,0:T(8,128)(2,1)S(1)} %pad_maximum_fusion.2), channel_id=1, replica_groups=mesh['y'=4,'z'=8,'x'=4,'c'=2] {'c'}, dimensions={0} | all-to-all | bytes 1441792 | tf_op jit(solution)/shard_map/all_to_all | solution.py:39
  324.6 12.8 %all-gather.7 = bf16[512,512]{1,0:T(8,128)(2,1)S(1)} all-gather(bf16[128,512]{1,0:T(8,128)(2,1)S(1)} %fusion.38), channel_id=9, replica_groups=mesh['y'=4,'z'=8,'x'=4,'c'=2] {'x'}, dimensions={0}, use_global_device_ids=true | all-gather | bytes 655360 | tf_op jit(solution)/shard_map/all_gather | solution.py:47
  338.6 4.4 %all_to_all.43 = bf16[2,8,176,128]{3,2,1,0:T(8,128)(2,1)S(1)} all-to-all(bf16[2,8,176,128]{3,2,1,0:T(8,128)(2,1)S(1)} %copy.412), channel_id=1, replica_groups=mesh['y'=4,'z'=8,'x'=4,'c'=2] {'c'}, dimensions={0} | all-to-all | bytes 1441792 | tf_op jit(solution)/shard_map/all_to_all | solution.py:39
  343.4 22.3 %all_to_all.44 = bf16[4,8,176,128]{3,2,1,0:T(8,128)(2,1)S(1)} all-to-all(bf16[4,8,176,128]{3,2,1,0:T(8,128)(2,1)S(1)} %pad_maximum_fusion), channel_id=1, replica_groups=mesh['y'=4,'z'=8,'x'=4,'c'=2] {'y'}, dimensions={0} | all-to-all | bytes 2883584 | tf_op jit(solution)/shard_map/all_to_all | solution.py:39
  366.0 17.5 %all_to_all.45 = bf16[8,176,128]{2,1,0:T(8,128)(2,1)S(1)} all-to-all(bf16[8,176,128]{2,1,0:T(8,128)(2,1)S(1)} %reduce_sum.294), channel_id=1, replica_groups=mesh['y'=4,'z'=8,'x'=4,'c'=2] {'z'}, dimensions={0} | all-to-all | bytes 720896 | tf_op jit(solution)/shard_map/all_to_all | solution.py:39
  (279 shorter events, 105.2 us)
Async XLA Ops:
  7.2 127.4 %all-gather.11.cloned.1.call-start = ((), (), s32[]{:S(2)}) async-start(), calls=%async_computation.8 | async-start | bytes 17039360 | tf_op jit(solution)/shard_map/all_gather | solution.py:73
  12.8 7.1 %copy-start.56 = (s32[2,2]{1,0:T(2,128)S(1)}, s32[2,2]{1,0:T(2,128)}, u32[]{:S(2)}) copy-start(s32[2,2]{1,0:T(2,128)} %param.16) | copy-start | bytes 52
  12.8 7.7 %copy-start.55 = (s32[4]{0:T(128)S(1)}, s32[4]{0:T(128)}, u32[]{:S(2)}) copy-start(s32[4]{0:T(128)} %param.17) | copy-start | bytes 52
  12.9 10.2 %copy-start.40 = (f32[1,8192]{1,0:T(1,128)S(1)}, f32[1,8192]{1,0:T(1,128)}, u32[]{:S(2)}) copy-start(f32[1,8192]{1,0:T(1,128)} %param.15) | copy-start | bytes 98308
  14.2 34.9 %all-to-all-start = ((bf16[4,2,32,2048]{3,2,1,0:T(8,128)(2,1)}), bf16[4,2,32,2048]{3,2,1,0:T(8,128)(2,1)S(1)}, u32[]{:S(2)}, u32[]{:S(2)}) async-start(bf16[4,2,32,2048]{3,2,1,0:T(8,128)(2,1)} %reshape.261), calls=%async_computation | async-start | bytes 2097152 | tf_op jit(solution)/shard_map/all_to_all | solution.py:39
  29.3 6.7 %copy-start.30 = (bf16[1,160,512]{2,1,0:T(8,128)(2,1)S(1)}, bf16[1,160,512]{2,1,0:T(8,128)(2,1)}, u32[]{:S(2)}) copy-start(bf16[1,160,512]{2,1,0:T(8,128)(2,1)} %param.14) | copy-start | bytes 491524
  49.0 128.2 %copy-start = (bf16[4,160,512]{2,1,0:T(8,128)(2,1)}, bf16[4,160,512]{2,1,0:T(8,128)(2,1)S(1)}, u32[]{:S(2)}) copy-start(bf16[4,160,512]{2,1,0:T(8,128)(2,1)S(1)} %all_gather.63) | copy-start | bytes 1966084
  50.9 64.7 %all-to-all-start.1 = ((bf16[4,160,2048]{2,1,0:T(8,128)(2,1)}), bf16[4,160,2048]{2,1,0:T(8,128)(2,1)}, u32[]{:S(2)}, u32[]{:S(2)}) async-start(bf16[4,160,2048]{2,1,0:T(8,128)(2,1)} %broadcast_in_dim.35), calls=%async_computation.1 | async-start | bytes 5242880 | tf_op jit(solution)/shard_map/all_to_all | solution.py:39
  113.0 41.9 %copy-start.35 = (f32[1,1,2048]{2,1,0:T(1,128)}, f32[1,1,2048]{2,1,0:T(1,128)S(1)}, u32[]{:S(2)}) copy-start(f32[1,1,2048]{2,1,0:T(1,128)S(1)} %get-tuple-element.35) | copy-start | bytes 24580
  113.0 64.2 %copy-start.36 = (f32[1,1,2048]{2,1,0:T(1,128)}, f32[1,1,2048]{2,1,0:T(1,128)S(1)}, u32[]{:S(2)}) copy-start(f32[1,1,2048]{2,1,0:T(1,128)S(1)} %get-tuple-element.37) | copy-start | bytes 24580
  115.6 21.2 %copy-start.5 = (bf16[4,1,32,2048]{3,2,1,0:T(8,128)(2,1)}, bf16[4,1,32,2048]{3,2,1,0:T(8,128)(2,1)S(1)}, u32[]{:S(2)}) copy-start(bf16[4,1,32,2048]{3,2,1,0:T(8,128)(2,1)S(1)} %get-tuple-element.10) | copy-start | bytes 1572868
  184.7 20.9 %copy-start.38 = (f32[1,1,2048]{2,1,0:T(1,128)S(1)}, f32[1,1,2048]{2,1,0:T(1,128)}, u32[]{:S(2)}) copy-start(f32[1,1,2048]{2,1,0:T(1,128)} %get-tuple-element.34) | copy-start | bytes 24580
  244.0 15.1 %copy-start.8 = (bf16[128,2048]{1,0:T(8,128)(2,1)}, bf16[128,2048]{1,0:T(8,128)(2,1)S(1)}, u32[]{:S(2)}) copy-start(bf16[128,2048]{1,0:T(8,128)(2,1)S(1)} %fusion.15) | copy-start | bytes 1572868
  244.0 16.2 %copy-start.1 = (bf16[4,160,512]{2,1,0:T(8,128)(2,1)S(1)}, bf16[4,160,512]{2,1,0:T(8,128)(2,1)}, u32[]{:S(2)}) copy-start(bf16[4,160,512]{2,1,0:T(8,128)(2,1)} %copy-done) | copy-start | bytes 1966084
  244.0 18.8 %copy-start.44 = (f32[128]{0:T(128)S(1)}, f32[128]{0:T(128)}, u32[]{:S(2)}) copy-start(f32[128]{0:T(128)} %copy-done.43) | copy-start | bytes 1540
  260.2 5.1 %copy-start.13 = (bf16[128,2048]{1,0:T(8,128)(2,1)S(1)}, bf16[128,2048]{1,0:T(8,128)(2,1)}, u32[]{:S(2)}) copy-start(bf16[128,2048]{1,0:T(8,128)(2,1)} %get-tuple-element.5) | copy-start | bytes 1572868
  268.0 15.1 %copy-start.7 = (bf16[128,2048]{1,0:T(8,128)(2,1)}, bf16[128,2048]{1,0:T(8,128)(2,1)S(1)}, u32[]{:S(2)}) copy-start(bf16[128,2048]{1,0:T(8,128)(2,1)S(1)} %fusion.16) | copy-start | bytes 1572868
  268.0 15.1 %copy-start.3 = (f32[128,802]{1,0:T(8,128)S(1)}, f32[128,802]{1,0:T(8,128)}, u32[]{:S(2)}) copy-start(f32[128,802]{1,0:T(8,128)} %copy-done.2) | copy-start | bytes 1231876
  268.0 15.8 %copy-start.20 = (f32[128,160]{0,1:T(8,128)S(1)}, f32[128,160]{0,1:T(8,128)}, u32[]{:S(2)}) copy-start(f32[128,160]{0,1:T(8,128)} %copy-done.19) | copy-start | bytes 245764
  268.1 18.0 %copy-start.42 = (f32[128]{0:T(128)S(1)}, f32[128]{0:T(128)}, u32[]{:S(2)}) copy-start(f32[128]{0:T(128)} %copy-done.41) | copy-start | bytes 1540
  321.9 15.7 %copy-start.10 = (bf16[2048,128]{1,0:T(8,128)(2,1)S(1)}, bf16[2048,128]{1,0:T(8,128)(2,1)}, u32[]{:S(2)}) copy-start(bf16[2048,128]{1,0:T(8,128)(2,1)} %copy.442) | copy-start | bytes 1572868
  321.9 15.7 %copy-start.48 = (f32[128]{0:T(128)S(1)}, f32[128]{0:T(128)}, u32[]{:S(2)}) copy-start(f32[128]{0:T(128)} %copy-done.47) | copy-start | bytes 1540
  324.6 13.6 %copy-start.24 = (bf16[128,160]{0,1:T(8,128)(2,1)S(1)}, bf16[128,160]{0,1:T(8,128)(2,1)}, u32[]{:S(2)}) copy-start(bf16[128,160]{0,1:T(8,128)(2,1)} %copy-done.23) | copy-start | bytes 122884
  338.5 4.8 %copy-start.16 = (bf16[8,176,128]{2,1,0:T(8,128)(2,1)S(1)}, bf16[8,176,128]{2,1,0:T(8,128)(2,1)}, u32[]{:S(2)}) copy-start(bf16[8,176,128]{2,1,0:T(8,128)(2,1)} %copy.471) | copy-start | bytes 1081348
  (36 other events, 119.3 us)
Sparse Core Ops, SparseCore 0:
  10.7 123.7 all-gather.10
where the time goes:
time: 394 us; the launch traced here: 392 us
  blocking collectives  222 us (56%)
  matrix products  56.4 us (14%)
  local copies, waits for them, and re-layouts  53.8 us (14%)
  waiting for transfers between devices  17.1 us (4%)
  other arithmetic  16.3 us (4%)
  between operations  16 us (4%)
  starting transfers between devices  10.3 us (3%)
    all_gather x7, blocking collectives, gathered_sum(): return summed(lax.all_gather(partial, 'x', axis=0, tiled=False))  94.5 us
    all_to_all x6, blocking collectives, exchanged(): return lax.all_to_all(value, axis, split_axis=0, concat_axis=0, tiled=True)  57.5 us
    dot_general x31, matrix products, contract(): lax.dot_general(left, right, (((left_dim,), (right_dim,)), ((), ())), pre...  56.4 us
    all_gather x1, blocking collectives, local(): gains = lax.all_gather(gains_local, 'y', axis=0, tiled=False)  44.8 us
    all_gather x1, waiting for transfers between devices, local(): full = lax.all_gather(joined, GROUP, axis=0, tiled=False)  17.1 us
    all_gather x1, blocking collectives, local(): ups = lax.all_gather(adapter_up_weight[0], 'y', axis=0, tiled=False)  13 us
    all_gather x1, blocking collectives, local(): lax.all_gather(jnp.broadcast_to(coef_row, (tokens, packed)), 'x', axis=0,...  12 us
    all_to_all x2, starting transfers between devices, exchanged(): return lax.all_to_all(value, axis, split_axis=0, concat_axis=0, tiled=True)  10.3 us
  transfers between devices with their start and end apart: 3, of which 1 were waited for; matrix products, arithmetic and copies ran while one was open for 7% of the time, Pallas kernels for 0%

commit v1 on v0

--- a/solution.py
+++ b/solution.py
@@ -99,7 +99,13 @@
     ups = lax.all_gather(adapter_up_weight[0], "y", axis=0, tiled=False)
     adapter = lax.dynamic_index_in_dim(segment_adapter_index.reshape(ny), yi, 0, keepdims=False)
     coef_row = coefficient_row(adapter, adapter_rank_blocks, packed)
-    coef = lax.all_gather(jnp.broadcast_to(coef_row, (tokens, packed)), "x", axis=0, tiled=True)
+
+    def remake_the_group(work_x, peer_axis):
+        b_next = jnp.stack([work_x for _ in range(lax.axis_size(peer_axis))])
+        passed = lax.all_to_all(b_next, peer_axis, split_axis=0, concat_axis=0)
+        return jnp.concatenate(passed, 0)
+
+    coef = remake_the_group(jnp.broadcast_to(coef_row, (tokens, packed)), "x")
     chunk = value_cols // layers
     last = contract(grad, out_full[layers - 1], 1, 0).astype(BF)
     inputs, scaled, projected, inverse, last_sum = ([], [], [], [], [])

time: 394 us -> 399 us (1.013)
  waiting for transfers between devices: 17.1 us -> 9.47 us
  blocking collectives: 222 us -> 227 us
  starting transfers between devices: 10.3 us -> 15.1 us
    all_gather x1, blocking collectives: 44.8 us -> 61.8 us  [local(): gains = lax.all_gather(gains_local, 'y', axis=0, tiled=False)]
    all_gather x1 -> x0, blocking collectives: 12 us -> none  [local(): lax.all_gather(jnp.broadcast_to(coef_row, (tokens, packed)), 'x', axis=0,...]
    all_gather x1, waiting for transfers between devices: 17.1 us -> 9.17 us  [local(): full = lax.all_gather(joined, GROUP, axis=0, tiled=False)]
    all_to_all x0 -> x1, starting transfers between devices: none -> 5.53 us  [remake_the_group(): passed = lax.all_to_all(b_next, peer_axis, split_axis=0, concat_axis=0)]
  transfers between devices with their start and end apart: 3 -> 4, of which waited for: 1 -> 2; matrix products, arithmetic and copies ran while one was open for 7% -> 7% of each run, Pallas kernels for 0% -> 0%
where the time goes in v1:
time: 399 us; the launch traced here: 396 us
  blocking collectives  227 us (57%)
  matrix products  56.4 us (14%)
  local copies, waits for them, and re-layouts  55.1 us (14%)
  other arithmetic  17 us (4%)
  between operations  15.9 us (4%)
  starting transfers between devices  15.1 us (4%)
  waiting for transfers between devices  9.47 us (2%)
    all_gather x7, blocking collectives, gathered_sum(): return summed(lax.all_gather(partial, 'x', axis=0, tiled=False))  95.4 us
    all_gather x1, blocking collectives, local(): gains = lax.all_gather(gains_local, 'y', axis=0, tiled=False)  61.8 us
    dot_general x31, matrix products, contract(): lax.dot_general(left, right, (((left_dim,), (right_dim,)), ((), ())), pre...  56.4 us
    all_to_all x6, blocking collectives, exchanged(): return lax.all_to_all(value, axis, split_axis=0, concat_axis=0, tiled=True)  56.2 us
    all_gather x1, blocking collectives, local(): ups = lax.all_gather(adapter_up_weight[0], 'y', axis=0, tiled=False)  13.8 us
    all_to_all x2, starting transfers between devices, exchanged(): return lax.all_to_all(value, axis, split_axis=0, concat_axis=0, tiled=True)  9.5 us
    all_gather x1, waiting for transfers between devices, local(): full = lax.all_gather(joined, GROUP, axis=0, tiled=False)  9.17 us
  transfers between devices with their start and end apart: 4, of which 2 were waited for; matrix products, arithmetic and copies ran while one was open for 7% of the time, Pallas kernels for 0%

profile of v1, /device:TPU:2, one launch (start us, length us, event | category | flops | bytes accessed | tf_op | source)
XLA Modules:
  0.0 396.2 jit_solution(16052977591796032692)
XLA Ops:
  15.4 5.5 %all-to-all-start.2 = ((f32[4,32,160]{2,1,0:T(8,128)}), f32[4,32,160]{2,1,0:T(8,128)S(1)}, u32[]{:S(2)}, u32[]{:S(2)}) async-start(f32[4,32,160]{2,1,0:T(8,128)} %stack.30), calls=%async_computation.2 | async-start | bytes 262144 | tf_op jit(solution)/shard_map/all_to_all | solution.py:105
  25.5 4.9 %all-to-all-start = ((bf16[4,2,32,2048]{3,2,1,0:T(8,128)(2,1)}), bf16[4,2,32,2048]{3,2,1,0:T(8,128)(2,1)S(1)}, u32[]{:S(2)}, u32[]{:S(2)}) async-start(bf16[4,2,32,2048]{3,2,1,0:T(8,128)(2,1)} %reshape.261), calls=%async_computation | async-start | bytes 2097152 | tf_op jit(solution)/shard_map/all_to_all | solution.py:39
  31.7 5.5 %reshape.264 = bf16[160,8,4,256]{3,2,1,0:T(4,128)(2,1)} reshape(bf16[160,8192]{1,0:T(8,128)(2,1)} %bitcast.316) | data formatting | bytes 5242880 | tf_op jit(solution)/shard_map/reshape | solution.py:92
  37.2 5.6 %dynamic-slice_reduce_fusion = bf16[160,8,256]{2,1,0:T(8,128)(2,1)S(1)} fusion(bf16[160,8,4,256]{3,2,1,0:T(4,128)(2,1)} %reshape.264, s32[]{:T(128)S(6)} %select_n.32), kind=kLoop, calls=%fused_computation.52 | loop fusion | bytes 1310724 | tf_op jit(solution)/shard_map/jit(dynamic_index_in_dim)/dynamic_slice | solution.py:91
  43.0 13.8 %all_gather.59 = bf16[4,160,512]{2,1,0:T(8,128)(2,1)S(1)} all-gather(bf16[1,160,512]{2,1,0:T(8,128)(2,1)S(1)} %copy-done.30), channel_id=1, replica_groups=mesh['y'=4,'z'=8,'x'=4,'c'=2] {'y'}, dimensions={0}, use_global_device_ids=true | all-gather | bytes 819200 | tf_op jit(solution)/shard_map/all_gather | solution.py:99
  58.6 4.6 %all-to-all-start.1 = ((bf16[4,160,2048]{2,1,0:T(8,128)(2,1)}), bf16[4,160,2048]{2,1,0:T(8,128)(2,1)}, u32[]{:S(2)}, u32[]{:S(2)}) async-start(bf16[4,160,2048]{2,1,0:T(8,128)(2,1)} %broadcast_in_dim.33), calls=%async_computation.1 | async-start | bytes 5242880 | tf_op jit(solution)/shard_map/all_to_all | solution.py:39
  63.2 61.8 %all-gather.8 = f32[4,1,2048]{2,1,0:T(1,128)S(1)} all-gather(f32[1,1,2048]{2,1,0:T(1,128)S(1)} %bitcast.355), channel_id=1, replica_groups=mesh['y'=4,'z'=8,'x'=4,'c'=2] {'y'}, dimensions={0}, use_global_device_ids=true | all-gather | bytes 40960 | tf_op jit(solution)/shard_map/all_gather | solution.py:98
  130.2 9.2 %all-gather.11.cloned.1.call-done = bf16[8192,1024]{1,0:T(8,128)(2,1)} async-done(((bf16[128,1024]{1,0:T(8,128)(2,1)}), bf16[8192,1024]{1,0:T(8,128)(2,1)}) %all-gather.11.cloned.1.call-update) | async-done | bytes 16777232 | tf_op jit(solution)/shard_map/all_gather | solution.py:73
  144.4 15.0 %all-gather.1 = bf16[512,802]{1,0:T(8,128)(2,1)S(1)} all-gather(bf16[128,802]{1,0:T(8,128)(2,1)S(1)} %concatenate.52), channel_id=3, replica_groups=mesh['y'=4,'z'=8,'x'=4,'c'=2] {'x'}, dimensions={0}, use_global_device_ids=true | all-gather | bytes 1026560 | tf_op jit(solution)/shard_map/all_gather | solution.py:47
  159.9 3.3 multiply_reduce_fusion.2
  167.5 13.8 %all-gather.2 = bf16[512,802]{1,0:T(8,128)(2,1)S(1)} all-gather(bf16[128,802]{1,0:T(8,128)(2,1)S(1)} %concatenate.53), channel_id=4, replica_groups=mesh['y'=4,'z'=8,'x'=4,'c'=2] {'x'}, dimensions={0}, use_global_device_ids=true | all-gather | bytes 1026560 | tf_op jit(solution)/shard_map/all_gather | solution.py:47
  182.3 3.4 multiply_reduce_fusion.1
  189.9 14.4 %all-gather.3 = bf16[512,802]{1,0:T(8,128)(2,1)S(1)} all-gather(bf16[128,802]{1,0:T(8,128)(2,1)S(1)} %concatenate.54), channel_id=5, replica_groups=mesh['y'=4,'z'=8,'x'=4,'c'=2] {'x'}, dimensions={0}, use_global_device_ids=true | all-gather | bytes 1026560 | tf_op jit(solution)/shard_map/all_gather | solution.py:47
  210.9 3.5 multiply_reduce_fusion
  222.0 13.6 %all-gather.4 = bf16[512,802]{1,0:T(8,128)(2,1)S(1)} all-gather(bf16[128,802]{1,0:T(8,128)(2,1)S(1)} %concatenate.55), channel_id=6, replica_groups=mesh['y'=4,'z'=8,'x'=4,'c'=2] {'x'}, dimensions={0}, use_global_device_ids=true | all-gather | bytes 1026560 | tf_op jit(solution)/shard_map/all_gather | solution.py:47
  251.5 12.8 %all-gather.5 = bf16[512,512]{1,0:T(8,128)(2,1)S(1)} all-gather(bf16[128,512]{1,0:T(8,128)(2,1)S(1)} %fusion.34), channel_id=7, replica_groups=mesh['y'=4,'z'=8,'x'=4,'c'=2] {'x'}, dimensions={0}, use_global_device_ids=true | all-gather | bytes 655360 | tf_op jit(solution)/shard_map/all_gather | solution.py:47
  275.6 12.8 %all-gather.6 = bf16[512,512]{1,0:T(8,128)(2,1)S(1)} all-gather(bf16[128,512]{1,0:T(8,128)(2,1)S(1)} %fusion.36), channel_id=8, replica_groups=mesh['y'=4,'z'=8,'x'=4,'c'=2] {'x'}, dimensions={0}, use_global_device_ids=true | all-gather | bytes 655360 | tf_op jit(solution)/shard_map/all_gather | solution.py:47
  296.5 4.3 %all_to_all.45 = bf16[2,8,176,128]{3,1,2,0:T(8,128)(2,1)S(1)} all-to-all(bf16[2,8,176,128]{3,1,2,0:T(8,128)(2,1)S(1)} %pad_maximum_fusion.4), channel_id=1, replica_groups=mesh['y'=4,'z'=8,'x'=4,'c'=2] {'c'}, dimensions={0} | all-to-all | bytes 1441792 | tf_op jit(solution)/shard_map/all_to_all | solution.py:39
  307.1 4.5 %all_to_all.46 = bf16[2,8,176,128]{3,1,2,0:T(8,128)(2,1)S(1)} all-to-all(bf16[2,8,176,128]{3,1,2,0:T(8,128)(2,1)S(1)} %pad_maximum_fusion.3), channel_id=1, replica_groups=mesh['y'=4,'z'=8,'x'=4,'c'=2] {'c'}, dimensions={0} | all-to-all | bytes 1441792 | tf_op jit(solution)/shard_map/all_to_all | solution.py:39
  319.4 4.3 %all_to_all.47 = bf16[2,8,176,128]{3,1,2,0:T(8,128)(2,1)S(1)} all-to-all(bf16[2,8,176,128]{3,1,2,0:T(8,128)(2,1)S(1)} %pad_maximum_fusion.2), channel_id=1, replica_groups=mesh['y'=4,'z'=8,'x'=4,'c'=2] {'c'}, dimensions={0} | all-to-all | bytes 1441792 | tf_op jit(solution)/shard_map/all_to_all | solution.py:39
  329.9 13.2 %all-gather.7 = bf16[512,512]{1,0:T(8,128)(2,1)S(1)} all-gather(bf16[128,512]{1,0:T(8,128)(2,1)S(1)} %fusion.38), channel_id=9, replica_groups=mesh['y'=4,'z'=8,'x'=4,'c'=2] {'x'}, dimensions={0}, use_global_device_ids=true | all-gather | bytes 655360 | tf_op jit(solution)/shard_map/all_gather | solution.py:47
  344.3 4.4 %all_to_all.48 = bf16[2,8,176,128]{3,2,1,0:T(8,128)(2,1)S(1)} all-to-all(bf16[2,8,176,128]{3,2,1,0:T(8,128)(2,1)S(1)} %copy.428), channel_id=1, replica_groups=mesh['y'=4,'z'=8,'x'=4,'c'=2] {'c'}, dimensions={0} | all-to-all | bytes 1441792 | tf_op jit(solution)/shard_map/all_to_all | solution.py:39
  349.2 22.3 %all_to_all.49 = bf16[4,8,176,128]{3,2,1,0:T(8,128)(2,1)S(1)} all-to-all(bf16[4,8,176,128]{3,2,1,0:T(8,128)(2,1)S(1)} %pad_maximum_fusion), channel_id=1, replica_groups=mesh['y'=4,'z'=8,'x'=4,'c'=2] {'y'}, dimensions={0} | all-to-all | bytes 2883584 | tf_op jit(solution)/shard_map/all_to_all | solution.py:39
  371.8 16.3 %all_to_all.50 = bf16[8,176,128]{2,1,0:T(8,128)(2,1)S(1)} all-to-all(bf16[8,176,128]{2,1,0:T(8,128)(2,1)S(1)} %reduce_sum.294), channel_id=1, replica_groups=mesh['y'=4,'z'=8,'x'=4,'c'=2] {'z'}, dimensions={0} | all-to-all | bytes 720896 | tf_op jit(solution)/shard_map/all_to_all | solution.py:39
  (276 shorter events, 107.5 us)
Async XLA Ops:
  7.2 132.2 %all-gather.11.cloned.1.call-start = ((), (), s32[]{:S(2)}) async-start(), calls=%async_computation.9 | async-start | bytes 17039360 | tf_op jit(solution)/shard_map/all_gather | solution.py:73
  15.4 10.1 %all-to-all-start.2 = ((f32[4,32,160]{2,1,0:T(8,128)}), f32[4,32,160]{2,1,0:T(8,128)S(1)}, u32[]{:S(2)}, u32[]{:S(2)}) async-start(f32[4,32,160]{2,1,0:T(8,128)} %stack.30), calls=%async_computation.2 | async-start | bytes 262144 | tf_op jit(solution)/shard_map/all_to_all | solution.py:105
  23.9 7.1 %copy-start.40 = (f32[1,8192]{1,0:T(1,128)S(1)}, f32[1,8192]{1,0:T(1,128)}, u32[]{:S(2)}) copy-start(f32[1,8192]{1,0:T(1,128)} %param.15) | copy-start | bytes 98308
  25.5 31.3 %all-to-all-start = ((bf16[4,2,32,2048]{3,2,1,0:T(8,128)(2,1)}), bf16[4,2,32,2048]{3,2,1,0:T(8,128)(2,1)S(1)}, u32[]{:S(2)}, u32[]{:S(2)}) async-start(bf16[4,2,32,2048]{3,2,1,0:T(8,128)(2,1)} %reshape.261), calls=%async_computation | async-start | bytes 2097152 | tf_op jit(solution)/shard_map/all_to_all | solution.py:39
  37.2 5.8 %copy-start.30 = (bf16[1,160,512]{2,1,0:T(8,128)(2,1)S(1)}, bf16[1,160,512]{2,1,0:T(8,128)(2,1)}, u32[]{:S(2)}) copy-start(bf16[1,160,512]{2,1,0:T(8,128)(2,1)} %param.14) | copy-start | bytes 491524
  56.8 125.5 %copy-start = (bf16[4,160,512]{2,1,0:T(8,128)(2,1)}, bf16[4,160,512]{2,1,0:T(8,128)(2,1)S(1)}, u32[]{:S(2)}) copy-start(bf16[4,160,512]{2,1,0:T(8,128)(2,1)S(1)} %all_gather.59) | copy-start | bytes 1966084
  58.6 69.7 %all-to-all-start.1 = ((bf16[4,160,2048]{2,1,0:T(8,128)(2,1)}), bf16[4,160,2048]{2,1,0:T(8,128)(2,1)}, u32[]{:S(2)}, u32[]{:S(2)}) async-start(bf16[4,160,2048]{2,1,0:T(8,128)(2,1)} %broadcast_in_dim.33), calls=%async_computation.1 | async-start | bytes 5242880 | tf_op jit(solution)/shard_map/all_to_all | solution.py:39
  125.6 34.3 %copy-start.35 = (f32[1,1,2048]{2,1,0:T(1,128)}, f32[1,1,2048]{2,1,0:T(1,128)S(1)}, u32[]{:S(2)}) copy-start(f32[1,1,2048]{2,1,0:T(1,128)S(1)} %get-tuple-element.35) | copy-start | bytes 24580
  125.6 56.7 %copy-start.36 = (f32[1,1,2048]{2,1,0:T(1,128)}, f32[1,1,2048]{2,1,0:T(1,128)S(1)}, u32[]{:S(2)}) copy-start(f32[1,1,2048]{2,1,0:T(1,128)S(1)} %get-tuple-element.37) | copy-start | bytes 24580
  128.3 13.3 %copy-start.5 = (bf16[4,1,32,2048]{3,2,1,0:T(8,128)(2,1)}, bf16[4,1,32,2048]{3,2,1,0:T(8,128)(2,1)S(1)}, u32[]{:S(2)}) copy-start(bf16[4,1,32,2048]{3,2,1,0:T(8,128)(2,1)S(1)} %get-tuple-element.10) | copy-start | bytes 1572868
  189.8 21.1 %copy-start.38 = (f32[1,1,2048]{2,1,0:T(1,128)S(1)}, f32[1,1,2048]{2,1,0:T(1,128)}, u32[]{:S(2)}) copy-start(f32[1,1,2048]{2,1,0:T(1,128)} %get-tuple-element.34) | copy-start | bytes 24580
  249.3 15.1 %copy-start.8 = (bf16[128,2048]{1,0:T(8,128)(2,1)}, bf16[128,2048]{1,0:T(8,128)(2,1)S(1)}, u32[]{:S(2)}) copy-start(bf16[128,2048]{1,0:T(8,128)(2,1)S(1)} %fusion.15) | copy-start | bytes 1572868
  249.3 16.2 %copy-start.1 = (bf16[4,160,512]{2,1,0:T(8,128)(2,1)S(1)}, bf16[4,160,512]{2,1,0:T(8,128)(2,1)}, u32[]{:S(2)}) copy-start(bf16[4,160,512]{2,1,0:T(8,128)(2,1)} %copy-done) | copy-start | bytes 1966084
  249.3 18.8 %copy-start.44 = (f32[128]{0:T(128)S(1)}, f32[128]{0:T(128)}, u32[]{:S(2)}) copy-start(f32[128]{0:T(128)} %copy-done.43) | copy-start | bytes 1540
  265.5 5.1 %copy-start.13 = (bf16[128,2048]{1,0:T(8,128)(2,1)S(1)}, bf16[128,2048]{1,0:T(8,128)(2,1)}, u32[]{:S(2)}) copy-start(bf16[128,2048]{1,0:T(8,128)(2,1)} %get-tuple-element.5) | copy-start | bytes 1572868
  273.3 15.1 %copy-start.7 = (bf16[128,2048]{1,0:T(8,128)(2,1)}, bf16[128,2048]{1,0:T(8,128)(2,1)S(1)}, u32[]{:S(2)}) copy-start(bf16[128,2048]{1,0:T(8,128)(2,1)S(1)} %fusion.16) | copy-start | bytes 1572868
  273.3 15.1 %copy-start.3 = (f32[128,802]{1,0:T(8,128)S(1)}, f32[128,802]{1,0:T(8,128)}, u32[]{:S(2)}) copy-start(f32[128,802]{1,0:T(8,128)} %copy-done.2) | copy-start | bytes 1231876
  273.3 15.8 %copy-start.20 = (f32[128,160]{0,1:T(8,128)S(1)}, f32[128,160]{0,1:T(8,128)}, u32[]{:S(2)}) copy-start(f32[128,160]{0,1:T(8,128)} %copy-done.19) | copy-start | bytes 245764
  273.4 18.0 %copy-start.42 = (f32[128]{0:T(128)S(1)}, f32[128]{0:T(128)}, u32[]{:S(2)}) copy-start(f32[128]{0:T(128)} %copy-done.41) | copy-start | bytes 1540
  327.2 16.1 %copy-start.10 = (bf16[2048,128]{1,0:T(8,128)(2,1)S(1)}, bf16[2048,128]{1,0:T(8,128)(2,1)}, u32[]{:S(2)}) copy-start(bf16[2048,128]{1,0:T(8,128)(2,1)} %copy.458) | copy-start | bytes 1572868
  327.2 16.1 %copy-start.48 = (f32[128]{0:T(128)S(1)}, f32[128]{0:T(128)}, u32[]{:S(2)}) copy-start(f32[128]{0:T(128)} %copy-done.47) | copy-start | bytes 1540
  329.9 14.0 %copy-start.24 = (bf16[128,160]{0,1:T(8,128)(2,1)S(1)}, bf16[128,160]{0,1:T(8,128)(2,1)}, u32[]{:S(2)}) copy-start(bf16[128,160]{0,1:T(8,128)(2,1)} %copy-done.23) | copy-start | bytes 122884
  344.2 4.8 %copy-start.16 = (bf16[8,176,128]{2,1,0:T(8,128)(2,1)S(1)}, bf16[8,176,128]{2,1,0:T(8,128)(2,1)}, u32[]{:S(2)}) copy-start(bf16[8,176,128]{2,1,0:T(8,128)(2,1)} %copy.487) | copy-start | bytes 1081348
  344.2 4.8 %copy-start.17 = (bf16[8,176,128]{2,1,0:T(8,128)(2,1)S(1)}, bf16[8,176,128]{2,1,0:T(8,128)(2,1)}, u32[]{:S(2)}) copy-start(bf16[8,176,128]{2,1,0:T(8,128)(2,1)} %copy.488) | copy-start | bytes 1081348
  (35 other events, 114.5 us)
Sparse Core Ops, SparseCore 0:
  10.7 128.5 all-gather.10
